TPU v7x, 128 devices: a whole 4x4x4 slice. The times are simulated.
128 devices in a mesh: chord: 8 (over y_lo, z), span: 16 (over x, y_hi, core).
Axes of the slice: x: 4, y: 4 (y_hi: 2, y_lo: 2; y = y_hi * 2 + y_lo), z: 4, core: 2. Of those that a mesh axis runs over, the one named last changes fastest.
Arguments:
- state: float32 [5, 125, 32, 32, 128], P(None, None, 'chord', 'span'), may hold values from -10 to 10
Outputs:
- residual: float32 [5, 125, 32, 32, 128], P(None, None, 'chord', 'span')
- viscosity: float32 [125, 32, 32, 128], P(None, 'chord', 'span')
All inputs are finite; a program needn't handle non-finite values.
Results may differ from a plain program's by a relative error of at most 0.0001.
Values sent between devices are 32-bit elements; how exact they have to be, the bound alone decides.
A program may use at most 128 MiB of HBM per device.

v0:
```python
import functools
import math

import jax
import jax.numpy as jnp
import numpy as np
from jax import lax
from jax.experimental import pallas as pl
from jax.experimental.pallas import tpu as pltpu
from jax.sharding import PartitionSpec as P

MESH = pl.DeviceIdType.MESH
EPS_SCALE = 0.01
SENSOR_CENTRE = -3.0
SENSOR_WIDTH = 1.5
RATIO_FLOOR = 1e-06
ENERGY_EPS = 1e-06
NODES = [-0.906179845938664, -0.5384693101056831, 0.0, 0.5384693101056831, 0.906179845938664]
WEIGHTS = [
    0.2369268850561891,
    0.4786286704993665,
    0.5688888888888889,
    0.4786286704993665,
    0.2369268850561891,
]


def legendre_values(points):
    values = [np.ones(points.shape), np.array(points)]
    for order in range(1, 5):
        values.append(
            ((2 * order + 1) * points * values[order] - order * values[order - 1]) / (order + 1)
        )
    return values


def tables():
    x = np.array(NODES)
    w = np.array(WEIGHTS)
    bary = np.array([1.0 / np.prod([x[j] - x[k] for k in range(5) if k != j]) for j in range(5)])
    deriv = np.zeros((5, 5))
    for i in range(5):
        for j in range(5):
            if i != j:
                deriv[i, j] = bary[j] / bary[i] / (x[i] - x[j])
        deriv[i, i] = -np.sum(deriv[i])
    left = np.ones(5)
    right = np.ones(5)
    for j in range(5):
        for k in range(5):
            if k != j:
                left[j] *= (-1.0 - x[k]) / (x[j] - x[k])
                right[j] *= (1.0 - x[k]) / (x[j] - x[k])
    legendre = legendre_values(x)
    fourth = 7.0 * legendre[3] + 3.0 * legendre[1]
    fifth = 9.0 * legendre[4] + 5.0 * legendre[2] + legendre[0]
    half_l = 0.25 * (fourth - fifth)
    half_r = 0.25 * (fourth + fifth)
    modal = np.zeros((5, 5))
    for k in range(5):
        modal[k, :] = w * math.sqrt((2 * k + 1) / 2.0) * legendre[k]
    own = deriv - np.outer(half_l, left) - np.outer(half_r, right)
    upper = (1.0 + x) / 2.0
    near = float(np.sum(right * half_r * upper))
    far = float(np.sum(right * half_r * (1.0 - upper)))
    return own, left, right, half_l, half_r, modal, upper, near, far


OWN, LEFT, RIGHT, HALF_L, HALF_R, MODAL, UPPER, K_NEAR, K_FAR = tables()


def even_odd(u):
    return u[0] + u[4], u[1] + u[3], u[0] - u[4], u[1] - u[3], u[2]


def line_traces(eo):
    s0, s1, d0, d1, m = eo
    even = (
        float((RIGHT[0] + RIGHT[4]) / 2) * s0
        + float((RIGHT[1] + RIGHT[3]) / 2) * s1
        + float(RIGHT[2]) * m
    )
    odd = float((RIGHT[0] - RIGHT[4]) / 2) * d0 + float((RIGHT[1] - RIGHT[3]) / 2) * d1
    return even - odd, even + odd


def line_apply(eo, prev, following):
    s0, s1, d0, d1, m = eo
    sp = prev + following
    dp = prev - following
    out = [None] * 5
    for i in (0, 1):
        a = [(OWN[i, j] + OWN[i, 4 - j]) / 2 for j in (0, 1)]
        b = [(OWN[i, j] - OWN[i, 4 - j]) / 2 for j in (0, 1)]
        p = (
            float(a[0]) * s0
            + float(a[1]) * s1
            + float(OWN[i, 2]) * m
            + float((HALF_L[i] + HALF_R[i]) / 2) * sp
        )
        q = float(b[0]) * d0 + float(b[1]) * d1 + float((HALF_L[i] - HALF_R[i]) / 2) * dp
        out[i] = p + q
        out[4 - i] = q - p
    b = [(OWN[2, j] - OWN[2, 4 - j]) / 2 for j in (0, 1)]
    out[2] = float(b[0]) * d0 + float(b[1]) * d1 + float((HALF_L[2] - HALF_R[2]) / 2) * dp
    return out


def modal_line(u):
    s0, s1, d0, d1, m = even_odd(u)
    out = []
    for k in range(5):
        if k % 2 == 0:
            out.append(
                float(MODAL[k, 0]) * s0 + float(MODAL[k, 1]) * s1 + float(MODAL[k, 2]) * m
            )
        else:
            out.append(float(MODAL[k, 0]) * d0 + float(MODAL[k, 1]) * d1)
    return out


def rows_roll(x, shift):
    return pltpu.roll(x, shift % 8, axis=x.ndim - 2)


def lanes_roll(x, shift):
    return pltpu.roll(x, shift % 128, axis=x.ndim - 1)


GROUPS = ((0, 2), (2, 4), (4, 5))
PAIRS = 63
SPOTS = tuple((dc, ds) for dc in (-1, 0, 1) for ds in (-1, 0, 1) if (dc, ds) != (0, 0))


def kernel(
    chords,
    spans,
    x_hbm,
    res_hbm,
    vis_hbm,
    u,
    gs,
    gc,
    gn,
    r,
    vis,
    modes,
    ts,
    tc,
    tsf,
    usr,
    usl,
    ucu,
    ucd,
    vsr,
    vsl,
    vcu,
    vcd,
    fsr,
    fsl,
    fcu,
    fcd,
    hsr,
    hsl,
    hcu,
    hcd,
    eps,
    eps_in,
    ks,
    kc,
    load_sem,
    out_sem,
    e_send,
    e_recv,
    u_send,
    u_recv,
    f_send,
    f_recv,
):
    c = lax.axis_index("chord")
    s = lax.axis_index("span")
    has_lo = c > 0
    has_hi = c < chords - 1
    s_of = {0: s, 1: lax.rem(s + 1, spans), -1: lax.rem(s + spans - 1, spans)}
    c_of = {0: c, 1: lax.rem(c + 1, chords), -1: lax.rem(c + chords - 1, chords)}

    def exists(dc):
        return {0: None, 1: has_hi, -1: has_lo}[dc]

    def guarded(cond, action):
        if cond is None:
            action()
        else:
            pl.when(cond)(action)

    barrier = pltpu.get_barrier_semaphore()
    for dc, ds in SPOTS:
        guarded(
            exists(dc),
            lambda dc=dc, ds=ds: pl.semaphore_signal(
                barrier, inc=1, device_id=(c_of[dc], s_of[ds]), device_id_type=MESH
            ),
        )

    loads = [pltpu.make_async_copy(x_hbm.at[v], u.at[v], load_sem.at[v]) for v in range(5)]
    for copy in loads:
        copy.start()

    row = lax.broadcasted_iota(jnp.int32, (8, 128), 0)
    lane = lax.broadcasted_iota(jnp.int32, (8, 128), 1)
    low_j = lax.rem(row, 2) == 0
    row_lo = row < 2
    row_hi = row >= 6
    first_lane = lane == 0
    last_lane = lane == 127

    def pick(mask, a, b):
        if a.ndim == 3:
            mask = jnp.broadcast_to(mask[None], a.shape)
        return jnp.where(mask, a, b)

    loads[0].wait()

    def modes_cb(a, carry):
        block = u[0, pl.ds(25 * a, 25)].reshape(5, 5, 8, 128)
        along_c = modal_line([block[:, k] for k in range(5)])
        stacked = [jnp.stack([along_c[o][b] for o in range(5)]) for b in range(5)]
        along_b = modal_line(stacked)
        for n in range(5):
            modes[pl.ds(25 * a + 5 * n, 5)] = along_b[n]
        return carry

    lax.fori_loop(0, 5, modes_cb, 0)
    low = jnp.zeros((4, 8, 128), jnp.float32)
    high = jnp.zeros((8, 128), jnp.float32)
    high4 = jnp.zeros((5, 8, 128), jnp.float32)
    for n in range(5):
        along_a = modal_line([modes[25 * a + 5 * n : 25 * a + 5 * n + 5] for a in range(5)])
        for m in range(5):
            square = along_a[m] * along_a[m]
            if n == 4 or m == 4:
                high4 = high4 + square
            else:
                low = low + square[:4]
                high = high + square[4]
    high = high + (high4[0] + high4[1]) + (high4[2] + high4[3]) + high4[4]
    total = (low[0] + low[1]) + (low[2] + low[3]) + high
    ratio = high / (total + ENERGY_EPS)
    level = jnp.log(jnp.maximum(ratio, RATIO_FLOOR)) * (1.0 / math.log(10.0))
    ramp = jnp.clip((level - SENSOR_CENTRE) / SENSOR_WIDTH, -1.0, 1.0)
    eps[...] = (EPS_SCALE * 0.5) * (1.0 + jnp.sin((0.5 * math.pi) * ramp))

    for v in range(1, 5):
        loads[v].wait()

    def local_ab(k, carry):
        v = k // 5
        a = k - 5 * v
        block = u[v, pl.ds(25 * a, 25)].reshape(5, 5, 8, 128)
        eo = even_odd([block[b] for b in range(5)])
        tl, tr = line_traces(eo)
        ts[pl.ds(25 * v + 5 * a, 5)] = pick(low_j, tl, tr)
        zero = jnp.zeros_like(tl)
        grad = line_apply(
            eo, pick(low_j, zero, rows_roll(tr, 1)), pick(low_j, rows_roll(tl, -1), zero)
        )
        for b in range(5):
            gs[v, pl.ds(25 * a + 5 * b, 5)] = grad[b]
        eo = even_odd([block[:, k] for k in range(5)])
        tl, tr = line_traces(eo)
        grad = line_apply(
            eo,
            pick(first_lane, tl, lanes_roll(tr, 1)),
            pick(last_lane, tr, lanes_roll(tl, -1)),
        )
        for b in range(5):
            gn[v, pl.ds(25 * a + 5 * b, 5)] = jnp.stack([grad[k][b] for k in range(5)])
        return carry

    lax.fori_loop(0, 25, local_ab, 0)

    def local_c(k, carry):
        v = k // 5
        b = k - 5 * v
        eo = even_odd([u[v, pl.ds(25 * a + 5 * b, 5)] for a in range(5)])
        tl, tr = line_traces(eo)
        q = 25 * v + 5 * b
        tc[pl.ds(q, 5)] = pick(row_lo, tl, tr)
        ucu[pl.ds(q, 5)] = tr[:, 6:8]
        ucd[pl.ds(q, 5)] = tl[:, 0:2]
        zero = jnp.zeros_like(tl)
        grad = line_apply(
            eo, pick(row_lo, zero, rows_roll(tr, 2)), pick(row_hi, zero, rows_roll(tl, -2))
        )
        for a in range(5):
            gc[v, pl.ds(25 * a + 5 * b, 5)] = grad[a]
        return carry

    lax.fori_loop(0, 25, local_c, 0)
    ts[125] = jnp.zeros((8, 128), jnp.float32)
    tsf[125] = jnp.zeros((8, 128), jnp.float32)

    def pack(src, to_right, to_left, start, count):
        def body(k, carry):
            p = start + k * 1
            two = src[pl.ds(2 * p, 2)]
            to_right[p] = jnp.where(low_j, rows_roll(two[0], -1), two[1])
            to_left[p] = jnp.where(low_j, two[0], rows_roll(two[1], 1))
            return carry

        lax.fori_loop(0, count, body, 0)

    def unpack(from_left, from_right, p):
        a, b = from_left[p], from_right[p]
        return (
            jnp.where(low_j, a, rows_roll(b, 1)),
            jnp.where(low_j, rows_roll(a, -1), b),
        )

    pack(ts, usr, usl, 0, PAIRS)

    pl.semaphore_wait(barrier, 2 + jnp.where(has_lo, 3, 0) + jnp.where(has_hi, 3, 0))

    eps_copies = []
    for k, (dc, ds) in enumerate(SPOTS):
        copy = pltpu.make_async_remote_copy(
            src_ref=eps,
            dst_ref=eps_in.at[k],
            send_sem=e_send.at[k],
            recv_sem=e_recv.at[k],
            device_id=(c_of[dc], s_of[ds]),
            device_id_type=MESH,
        )
        guarded(exists(dc), copy.start)
        eps_copies.append((dc, ds, copy))

    def exchange(bufs, sems, g):
        (sr, sl, cu, cd), (dr, dl, du, dd) = bufs
        v0, v1 = GROUPS[g]
        pairs = pl.ds(25 * v0 // 2, -(-25 * (v1 - v0) // 2))
        lines = pl.ds(25 * v0, 25 * (v1 - v0))
        out = []
        for k, (src, dst, dc, ds, part) in enumerate(
            (
                (sr, dr, 0, 1, pairs),
                (sl, dl, 0, -1, pairs),
                (cu, du, 1, 0, lines),
                (cd, dd, -1, 0, lines),
            )
        ):
            copy = pltpu.make_async_remote_copy(
                src_ref=src.at[part],
                dst_ref=dst.at[part],
                send_sem=sems[0].at[4 * g + k],
                recv_sem=sems[1].at[4 * g + k],
                device_id=(c_of[dc], s_of[ds]),
                device_id_type=MESH,
            )
            out.append((dc, copy))
        return out

    u_copies = [
        exchange(((usr, usl, ucu, ucd), (vsr, vsl, vcu, vcd)), (u_send, u_recv), g)
        for g in range(3)
    ]
    f_copies = [
        exchange(((fsr, fsl, fcu, fcd), (hsr, hsl, hcu, hcd)), (f_send, f_recv), g)
        for g in range(3)
    ]

    def start(copies):
        for dc, copy in copies:
            guarded(exists(dc), copy.start)

    def arrive(copies):
        for dc, copy in copies:
            guarded(exists(-dc), copy.wait_recv)

    def sent(copies):
        for dc, copy in copies:
            guarded(exists(dc), copy.wait_send)

    for g in range(3):
        start(u_copies[g])

    for dc, ds, copy in eps_copies:
        guarded(exists(-dc), copy.wait_recv)

    around = {(0, 0): eps[...]}
    for k, (dc, ds) in enumerate(SPOTS):
        value = eps_in[k]
        cond = exists(-dc)
        if cond is not None:
            value = jnp.where(cond, value, jnp.zeros_like(value))
        around[(-dc, -ds)] = value
    faces = {}
    for dc in (-1, 0, 1):
        mid, left, right = around[(dc, 0)], around[(dc, -1)], around[(dc, 1)]
        before = jnp.where(low_j, rows_roll(left, -1), rows_roll(mid, 1))
        after = jnp.where(low_j, rows_roll(mid, -1), rows_roll(right, 1))
        beyond = jnp.where(low_j, left, right)
        faces[dc] = (
            jnp.maximum(before, mid),
            jnp.maximum(mid, after),
            jnp.maximum(beyond, jnp.where(low_j, before, after)),
        )

    def normal_pair(x):
        zero = jnp.zeros_like(x)
        return (
            jnp.maximum(x, jnp.where(first_lane, zero, lanes_roll(x, 1))),
            jnp.maximum(x, jnp.where(last_lane, zero, lanes_roll(x, -1))),
        )

    corner = {}
    span_far = {}
    chord_far = {}
    for k in range(3):
        below, mid, above = faces[-1][k], faces[0][k], faces[1][k]
        before = jnp.where(row_lo, rows_roll(below, 2), rows_roll(mid, 2))
        after = jnp.where(row_hi, rows_roll(above, -2), rows_roll(mid, -2))
        for sx, value in ((0, jnp.maximum(before, mid)), (1, jnp.maximum(mid, after))):
            pair = normal_pair(value)
            for sz in range(2):
                if k == 2:
                    span_far[(sx, sz)] = pair[sz]
                else:
                    corner[(sx, k, sz)] = pair[sz]
        if k < 2:
            beyond = jnp.where(row_lo, rows_roll(below, 4), rows_roll(above, 4))
            pair = normal_pair(jnp.maximum(beyond, jnp.where(row_lo, before, after)))
            for sz in range(2):
                chord_far[(k, sz)] = pair[sz]

    def between(lo, hi):
        step = hi - lo
        return [lo + float(UPPER[i]) * step for i in range(5)]

    plane = {
        (sy, sz): between(corner[(0, sy, sz)], corner[(1, sy, sz)])
        for sy in range(2)
        for sz in range(2)
    }
    for a in range(5):
        edge = [between(plane[(0, sz)][a], plane[(1, sz)][a]) for sz in range(2)]
        for b in range(5):
            vis[pl.ds(25 * a + 5 * b, 5)] = jnp.stack(between(edge[0][b], edge[1][b]))
    vis_copy = pltpu.make_async_copy(vis, vis_hbm, out_sem.at[5])
    vis_copy.start()
    weight = {}
    for sx in range(2):
        for sz in range(2):
            near = jnp.where(low_j, corner[(sx, 0, sz)], corner[(sx, 1, sz)])
            value = K_FAR * span_far[(sx, sz)] + K_NEAR * near
            weight[(sx, sz)] = jnp.where(low_j, value, -value)
    edge = [between(weight[(0, sz)], weight[(1, sz)]) for sz in range(2)]
    for a in range(5):
        ks[pl.ds(5 * a, 5)] = jnp.stack(between(edge[0][a], edge[1][a]))
    for sy in range(2):
        for sz in range(2):
            near = jnp.where(row_lo, corner[(0, sy, sz)], corner[(1, sy, sz)])
            value = K_FAR * chord_far[(sy, sz)] + K_NEAR * near
            weight[(sy, sz)] = jnp.where(row_lo, value, -value)
    edge = [between(weight[(0, sz)], weight[(1, sz)]) for sz in range(2)]
    for b in range(5):
        kc[pl.ds(5 * b, 5)] = jnp.stack(between(edge[0][b], edge[1][b]))

    span_trace = [jnp.where(low_j, float(LEFT[b]), float(RIGHT[b])) for b in range(5)]
    chord_trace = [jnp.where(row_lo, float(LEFT[a]), float(RIGHT[a])) for a in range(5)]
    span_lift = [jnp.where(low_j, float(HALF_L[b]), float(HALF_R[b])) for b in range(5)]
    chord_lift = [
        jnp.where(row_lo, float(HALF_L[a]), jnp.where(row_hi, float(HALF_R[a]), 0.0))
        for a in range(5)
    ]

    def flux_traces(k, carry):
        v = k // 5
        a = k - 5 * v
        at = [pl.ds(25 * a + 5 * b, 5) for b in range(5)]
        acc = None
        for b in range(5):
            term = span_trace[b][None] * (vis[at[b]] * gs[v, at[b]])
            acc = term if acc is None else acc + term
        tsf[pl.ds(25 * v + 5 * a, 5)] = acc
        at = [pl.ds(25 * i + 5 * a, 5) for i in range(5)]
        acc = None
        for i in range(5):
            term = chord_trace[i][None] * (vis[at[i]] * gc[v, at[i]])
            acc = term if acc is None else acc + term
        q = 25 * v + 5 * a
        fcu[pl.ds(q, 5)] = acc[:, 6:8]
        fcd[pl.ds(q, 5)] = acc[:, 0:2]
        return carry

    for g, (v0, v1) in enumerate(GROUPS):
        lax.fori_loop(5 * v0, 5 * v1, flux_traces, 0)
        pack(tsf, fsr, fsl, 25 * v0 // 2, -(-25 * (v1 - v0) // 2))
        start(f_copies[g])

    def normal_part(k, carry):
        v = k // 5
        a = k - 5 * v
        block = gn[v, pl.ds(25 * a, 25)] * vis[pl.ds(25 * a, 25)]
        block = block.reshape(5, 5, 8, 128)
        eo = even_odd([block[:, i] for i in range(5)])
        tl, tr = line_traces(eo)
        out = line_apply(
            eo,
            pick(first_lane, -tl, lanes_roll(tr, 1)),
            pick(last_lane, -tr, lanes_roll(tl, -1)),
        )
        for b in range(5):
            r[v, pl.ds(25 * a + 5 * b, 5)] = jnp.stack([out[i][b] for i in range(5)])
        return carry

    lax.fori_loop(0, 25, normal_part, 0)

    end_lo = jnp.logical_and(row_lo, jnp.logical_not(has_lo))
    end_hi = jnp.logical_and(row_hi, jnp.logical_not(has_hi))

    def unpack_all(from_left, from_right, dst, start_pair, count):
        def body(k, carry):
            p = start_pair + k
            first, second = unpack(from_left, from_right, p)
            dst[2 * p] = first
            dst[2 * p + 1] = second
            return carry

        lax.fori_loop(0, count, body, 0)

    def chord_outer(from_lo, from_hi, q):
        lo = from_lo[pl.ds(q, 5)]
        hi = from_hi[pl.ds(q, 5)]
        gap = jnp.zeros((5, 4, 128), jnp.float32)
        return jnp.concatenate([lo, gap, hi], axis=1)

    def span_part(k, carry):
        v = k // 5
        a = k - 5 * v
        outer = tsf[pl.ds(25 * v + 5 * a, 5)]
        flux = [
            vis[pl.ds(25 * a + 5 * b, 5)]
            * (gs[v, pl.ds(25 * a + 5 * b, 5)] + span_lift[b][None] * outer)
            for b in range(5)
        ]
        eo = even_odd(flux)
        tl, tr = line_traces(eo)
        zero = jnp.zeros_like(tl)
        out = line_apply(
            eo, pick(low_j, zero, rows_roll(tr, 1)), pick(low_j, rows_roll(tl, -1), zero)
        )
        for b in range(5):
            at = pl.ds(25 * a + 5 * b, 5)
            r[v, at] = r[v, at] + out[b]
        return carry

    def chord_part(k, carry):
        v = k // 5
        b = k - 5 * v
        q = 25 * v + 5 * b
        own = tc[pl.ds(q, 5)]
        outer = chord_outer(vcu, vcd, q)
        outer = pick(jnp.logical_or(end_lo, end_hi), own, outer)
        flux = [
            vis[pl.ds(25 * a + 5 * b, 5)]
            * (gc[v, pl.ds(25 * a + 5 * b, 5)] + chord_lift[a][None] * outer)
            for a in range(5)
        ]
        eo = even_odd(flux)
        tl, tr = line_traces(eo)
        zero = jnp.zeros_like(tl)
        out = line_apply(
            eo,
            pick(row_lo, pick(end_lo, -tl, zero), rows_roll(tr, 2)),
            pick(row_hi, pick(end_hi, -tr, zero), rows_roll(tl, -2)),
        )
        for a in range(5):
            at = pl.ds(25 * a + 5 * b, 5)
            r[v, at] = r[v, at] + out[a]
        return carry

    for g, (v0, v1) in enumerate(GROUPS):
        arrive(u_copies[g])
        unpack_all(vsr, vsl, tsf, 25 * v0 // 2, -(-25 * (v1 - v0) // 2))
        lax.fori_loop(5 * v0, 5 * v1, span_part, 0)
        lax.fori_loop(5 * v0, 5 * v1, chord_part, 0)

    def finish(k, carry):
        v = k // 5
        a = k - 5 * v
        q = 25 * v + 5 * a
        outer = tsf[pl.ds(q, 5)] + ks[pl.ds(5 * a, 5)] * ts[pl.ds(q, 5)]
        for b in range(5):
            at = pl.ds(25 * a + 5 * b, 5)
            r[v, at] = r[v, at] + span_lift[b][None] * outer
        return carry

    def finish_chord(k, carry):
        v = k // 5
        b = k - 5 * v
        q = 25 * v + 5 * b
        outer = chord_outer(hcu, hcd, q) + kc[pl.ds(5 * b, 5)] * tc[pl.ds(q, 5)]
        outer = pick(jnp.logical_or(end_lo, end_hi), jnp.zeros_like(outer), outer)
        for a in range(5):
            at = pl.ds(25 * a + 5 * b, 5)
            r[v, at] = r[v, at] + chord_lift[a][None] * outer
        return carry

    outs = [vis_copy]
    for g, (v0, v1) in enumerate(GROUPS):
        arrive(f_copies[g])
        unpack_all(hsr, hsl, tsf, 25 * v0 // 2, -(-25 * (v1 - v0) // 2))
        lax.fori_loop(5 * v0, 5 * v1, finish, 0)
        lax.fori_loop(5 * v0, 5 * v1, finish_chord, 0)
        copy = pltpu.make_async_copy(
            r.at[pl.ds(v0, v1 - v0)], res_hbm.at[pl.ds(v0, v1 - v0)], out_sem.at[g]
        )
        copy.start()
        outs.append(copy)
    for dc, ds, copy in eps_copies:
        guarded(exists(dc), copy.wait_send)
    for g in range(3):
        sent(u_copies[g])
        sent(f_copies[g])
    for copy in outs:
        copy.wait()


def shards(state):
    chords, spans = lax.axis_size("chord"), lax.axis_size("span")
    f32 = jnp.float32
    field = pltpu.VMEM((5, 125, 8, 128), f32)
    pairs = pltpu.VMEM((PAIRS, 8, 128), f32)
    thin = pltpu.VMEM((132, 2, 128), f32)
    sem = pltpu.SemaphoreType.DMA
    residual, viscosity = pl.pallas_call(
        functools.partial(kernel, chords, spans),
        out_shape=(
            jax.ShapeDtypeStruct((5, 125, 8, 128), f32),
            jax.ShapeDtypeStruct((125, 8, 128), f32),
        ),
        in_specs=[pl.BlockSpec(memory_space=pl.ANY)],
        out_specs=(pl.BlockSpec(memory_space=pl.ANY), pl.BlockSpec(memory_space=pl.ANY)),
        scratch_shapes=[
            field,
            field,
            field,
            field,
            field,
            pltpu.VMEM((125, 8, 128), f32),
            pltpu.VMEM((125, 8, 128), f32),
            pltpu.VMEM((126, 8, 128), f32),
            pltpu.VMEM((125, 8, 128), f32),
            pltpu.VMEM((126, 8, 128), f32),
        ]
        + [pairs, pairs, thin, thin] * 4
        + [
            pltpu.VMEM((8, 128), f32),
            pltpu.VMEM((8, 8, 128), f32),
            pltpu.VMEM((25, 8, 128), f32),
            pltpu.VMEM((25, 8, 128), f32),
            sem((5,)),
            sem((6,)),
            sem((8,)),
            sem((8,)),
            sem((12,)),
            sem((12,)),
            sem((12,)),
            sem((12,)),
        ],
        compiler_params=pltpu.CompilerParams(
            collective_id=0, has_side_effects=True, vmem_limit_bytes=56 * 1024 * 1024
        ),
        name="viscous",
    )(state.reshape(5, 125, 8, 128))
    return residual.reshape(state.shape), viscosity.reshape(state.shape[1:])


def solution(mesh):
    in_specs = (P(None, None, "chord", "span", None),)
    out_specs = (P(None, None, "chord", "span", None), P(None, "chord", "span", None))
    return jax.shard_map(shards, mesh=mesh, in_specs=in_specs, out_specs=out_specs, check_vma=False)
```

profile of v0, /device:TPU:24, one launch (start us, length us, event | category | flops | bytes accessed | tf_op | source)
XLA Modules:
  0.0 36.0 jit_solution(8811034981920206555)
XLA Ops:
  0.6 30.4 %viscous.1 = (f32[5,125,8,128]{3,2,1,0:T(8,128)}, f32[125,8,128]{2,1,0:T(8,128)}) custom-call(f32[5,125,8,128]{3,2,1,0:T(8,128)} %bitcast.3), custom_call_target="tpu_custom_call" | custom-call | tf_op jit(solution)/shard_map/viscous/pallas_call | solution.py:636
  31.1 0.0 copy-start
  31.1 4.1 %copy.5 = f32[5,125,4,2,128]{4,3,2,1,0:T(2,128)} copy(f32[5,125,4,2,128]{4,3,2,1,0:T(2,128)} %bitcast.4) | data formatting | bytes 5120000
  35.2 0.0 copy-done
  35.2 0.8 %copy.6 = f32[125,4,2,128]{3,2,1,0:T(2,128)} copy(f32[125,4,2,128]{3,2,1,0:T(2,128)S(1)} %bitcast.5) | data formatting | bytes 1024000
Async XLA Ops:
  31.1 4.1 %copy-start = (f32[125,8,128]{2,1,0:T(8,128)S(1)}, f32[125,8,128]{2,1,0:T(8,128)}, u32[]{:S(2)}) copy-start(f32[125,8,128]{2,1,0:T(8,128)} %get-tuple-element.5) | copy-start | bytes 1536004
where the time goes:
time: 36.2 us; the launch traced here: 36 us
  Pallas kernels  30.4 us (84%)
  local copies, waits for them, and re-layouts  4.92 us (14%)
  between operations  0.65 us (2%)
    pallas_call x1, Pallas kernels, shards(): pl.pallas_call(functools.partial(kernel, chords, spans), out_shape=(jax.S...  30.4 us
    unnamed x4, local copies, waits for them, and re-layouts  4.92 us

commit v1 on v0

--- a/solution.py
+++ b/solution.py
@@ -136,14 +136,12 @@
     chords,
     spans,
     x_hbm,
-    res_hbm,
-    vis_hbm,
+    r,
+    vis,
     u,
     gs,
     gc,
     gn,
-    r,
-    vis,
     modes,
     ts,
     tc,
@@ -169,7 +167,6 @@
     ks,
     kc,
     load_sem,
-    out_sem,
     e_send,
     e_recv,
     u_send,
@@ -445,8 +442,6 @@
         edge = [between(plane[(0, sz)][a], plane[(1, sz)][a]) for sz in range(2)]
         for b in range(5):
             vis[pl.ds(25 * a + 5 * b, 5)] = jnp.stack(between(edge[0][b], edge[1][b]))
-    vis_copy = pltpu.make_async_copy(vis, vis_hbm, out_sem.at[5])
-    vis_copy.start()
     weight = {}
     for sx in range(2):
         for sz in range(2):
@@ -606,23 +601,25 @@
             r[v, at] = r[v, at] + chord_lift[a][None] * outer
         return carry
 
-    outs = [vis_copy]
     for g, (v0, v1) in enumerate(GROUPS):
         arrive(f_copies[g])
         unpack_all(hsr, hsl, tsf, 25 * v0 // 2, -(-25 * (v1 - v0) // 2))
         lax.fori_loop(5 * v0, 5 * v1, finish, 0)
         lax.fori_loop(5 * v0, 5 * v1, finish_chord, 0)
-        copy = pltpu.make_async_copy(
-            r.at[pl.ds(v0, v1 - v0)], res_hbm.at[pl.ds(v0, v1 - v0)], out_sem.at[g]
-        )
-        copy.start()
-        outs.append(copy)
     for dc, ds, copy in eps_copies:
         guarded(exists(dc), copy.wait_send)
     for g in range(3):
         sent(u_copies[g])
         sent(f_copies[g])
-    for copy in outs:
+
+
+def store_kernel(r, vis, res_hbm, vis_hbm, sem):
+    copies = [
+        pltpu.make_async_copy(r.at[v], res_hbm.at[v], sem.at[v]) for v in range(5)
+    ] + [pltpu.make_async_copy(vis, vis_hbm, sem.at[5])]
+    for copy in copies:
+        copy.start()
+    for copy in copies:
         copy.wait()
 
 
@@ -633,21 +630,19 @@
     pairs = pltpu.VMEM((PAIRS, 8, 128), f32)
     thin = pltpu.VMEM((132, 2, 128), f32)
     sem = pltpu.SemaphoreType.DMA
-    residual, viscosity = pl.pallas_call(
+    partial, viscosity = pl.pallas_call(
         functools.partial(kernel, chords, spans),
         out_shape=(
             jax.ShapeDtypeStruct((5, 125, 8, 128), f32),
             jax.ShapeDtypeStruct((125, 8, 128), f32),
         ),
-        in_specs=[pl.BlockSpec(memory_space=pl.ANY)],
-        out_specs=(pl.BlockSpec(memory_space=pl.ANY), pl.BlockSpec(memory_space=pl.ANY)),
+        in_specs=[pl.BlockSpec(memory_space=pltpu.HBM)],
+        out_specs=(pl.BlockSpec(memory_space=pltpu.VMEM), pl.BlockSpec(memory_space=pltpu.VMEM)),
         scratch_shapes=[
             field,
             field,
             field,
             field,
-            field,
-            pltpu.VMEM((125, 8, 128), f32),
             pltpu.VMEM((125, 8, 128), f32),
             pltpu.VMEM((126, 8, 128), f32),
             pltpu.VMEM((125, 8, 128), f32),
@@ -660,7 +655,6 @@
             pltpu.VMEM((25, 8, 128), f32),
             pltpu.VMEM((25, 8, 128), f32),
             sem((5,)),
-            sem((6,)),
             sem((8,)),
             sem((8,)),
             sem((12,)),
@@ -669,10 +663,22 @@
             sem((12,)),
         ],
         compiler_params=pltpu.CompilerParams(
-            collective_id=0, has_side_effects=True, vmem_limit_bytes=56 * 1024 * 1024
+            collective_id=0, has_side_effects=True, vmem_limit_bytes=40 * 1024 * 1024
         ),
         name="viscous",
-    )(state.reshape(5, 125, 8, 128))
+    )(pltpu.with_memory_space_constraint(state.reshape(5, 125, 8, 128), pltpu.HBM))
+    residual, viscosity = pl.pallas_call(
+        store_kernel,
+        out_shape=(
+            jax.ShapeDtypeStruct((5, 125, 8, 128), f32),
+            jax.ShapeDtypeStruct((125, 8, 128), f32),
+        ),
+        in_specs=[pl.BlockSpec(memory_space=pltpu.VMEM)] * 2,
+        out_specs=(pl.BlockSpec(memory_space=pl.ANY), pl.BlockSpec(memory_space=pl.ANY)),
+        scratch_shapes=[sem((6,))],
+        compiler_params=pltpu.CompilerParams(vmem_limit_bytes=4 * 1024 * 1024),
+        name="store",
+    )(partial, viscosity)
     return residual.reshape(state.shape), viscosity.reshape(state.shape[1:])
 
 

time: 36.2 us -> 32.1 us (0.89)
  local copies, waits for them, and re-layouts: 4.92 us -> 0 us
  Pallas kernels: 30.4 us -> 31.3 us
    unnamed x4 -> x0, local copies, waits for them, and re-layouts: 4.92 us -> none
    pallas_call x0 -> x1, Pallas kernels: none -> 1.68 us  [shards(): pl.pallas_call(store_kernel, out_shape=(jax.ShapeDtypeStruct((5, 125, 8,...]
    pallas_call x1, Pallas kernels: 30.4 us -> 29.6 us  [shards(): pl.pallas_call(functools.partial(kernel, chords, spans), out_shape=(jax.S...]
where the time goes in v1:
time: 32.1 us; the launch traced here: 31.9 us
  Pallas kernels  31.3 us (98%)
  between operations  0.64 us (2%)
    pallas_call x1, Pallas kernels, shards(): pl.pallas_call(functools.partial(kernel, chords, spans), out_shape=(jax.S...  29.6 us
    pallas_call x1, Pallas kernels, shards(): pl.pallas_call(store_kernel, out_shape=(jax.ShapeDtypeStruct((5, 125, 8,...  1.68 us

profile of v1, /device:TPU:24, one launch (start us, length us, event | category | flops | bytes accessed | tf_op | source)
XLA Modules:
  0.0 31.9 jit_solution(14776183692207671550)
XLA Ops:
  0.6 29.6 %viscous.1 = (f32[5,125,8,128]{3,2,1,0:T(8,128)S(1)}, f32[125,8,128]{2,1,0:T(8,128)S(1)}) custom-call(f32[5,125,8,128]{3,2,1,0:T(8,128)} %bitcast.3), custom_call_target="tpu_custom_call" | custom-call | tf_op jit(solution)/shard_map/viscous/pallas_call | solution.py:633
  30.3 1.7 %store.1 = (f32[5,125,8,128]{3,2,1,0:T(8,128)}, f32[125,8,128]{2,1,0:T(8,128)}) custom-call(f32[5,125,8,128]{3,2,1,0:T(8,128)S(1)} %get-tuple-element.6.r, f32[125,8,128]{2,1,0:T(8,128)S(1)} %get-tuple-element.7.vis), custom_call_target="tpu_custom_call" | custom-call | tf_op jit(solution)/shard_map/store/pallas_call | solution.py:670

commit v2 on v1

--- a/solution.py
+++ b/solution.py
@@ -129,6 +129,8 @@
 
 GROUPS = ((0, 2), (2, 4), (4, 5))
 PAIRS = 63
+ROUTES = {("u", 0): 0, ("u", 1): 1, ("u", 2): 2}
+RELAYS = tuple(ROUTES)
 SPOTS = tuple((dc, ds) for dc in (-1, 0, 1) for ds in (-1, 0, 1) if (dc, ds) != (0, 0))
 
 
@@ -162,6 +164,7 @@
     hsl,
     hcu,
     hcd,
+    held,
     eps,
     eps_in,
     ks,
@@ -173,6 +176,8 @@
     u_recv,
     f_send,
     f_recv,
+    h_send,
+    h_recv,
 ):
     c = lax.axis_index("chord")
     s = lax.axis_index("span")
@@ -198,6 +203,33 @@
                 barrier, inc=1, device_id=(c_of[dc], s_of[ds]), device_id_type=MESH
             ),
         )
+
+    half = chords // 2
+    is_up = c == half - 1
+    is_down = c == half
+    stations = sorted(set(ROUTES.values()))
+
+    def meet(cond, others):
+        for other in others:
+            pl.when(cond)(
+                lambda other=other: pl.semaphore_signal(
+                    barrier, inc=1, device_id=(other, s), device_id_type=MESH
+                )
+            )
+        return jnp.where(cond, len(others), 0)
+
+    last = chords - 1
+    extra = 0
+    for at, others in (
+        (half - 1, [t for t in stations if t != half - 2] + [last - t for t in stations]),
+        (half, [last - t for t in stations if t != half - 2] + [t for t in stations]),
+    ):
+        extra = extra + meet(c == at, others)
+    for t in stations:
+        near = [] if t == half - 2 else [half - 1]
+        extra = extra + meet(c == t, near + [half])
+        near = [] if t == half - 2 else [half]
+        extra = extra + meet(c == last - t, near + [half - 1])
 
     loads = [pltpu.make_async_copy(x_hbm.at[v], u.at[v], load_sem.at[v]) for v in range(5)]
     for copy in loads:
@@ -250,73 +282,50 @@
     for v in range(1, 5):
         loads[v].wait()
 
-    def local_ab(k, carry):
-        v = k // 5
-        a = k - 5 * v
-        block = u[v, pl.ds(25 * a, 25)].reshape(5, 5, 8, 128)
-        eo = even_odd([block[b] for b in range(5)])
-        tl, tr = line_traces(eo)
-        ts[pl.ds(25 * v + 5 * a, 5)] = pick(low_j, tl, tr)
-        zero = jnp.zeros_like(tl)
-        grad = line_apply(
-            eo, pick(low_j, zero, rows_roll(tr, 1)), pick(low_j, rows_roll(tl, -1), zero)
-        )
+    span_trace = [jnp.where(low_j, float(LEFT[b]), float(RIGHT[b])) for b in range(5)]
+    chord_trace = [jnp.where(row_lo, float(LEFT[a]), float(RIGHT[a])) for a in range(5)]
+    span_lift = [jnp.where(low_j, float(HALF_L[b]), float(HALF_R[b])) for b in range(5)]
+    chord_lift = [
+        jnp.where(row_lo, float(HALF_L[a]), jnp.where(row_hi, float(HALF_R[a]), 0.0))
+        for a in range(5)
+    ]
+
+    def outer_traces(k, carry):
+        v = k // 5
+        i = k - 5 * v
+        q = 25 * v + 5 * i
+        acc = None
         for b in range(5):
-            gs[v, pl.ds(25 * a + 5 * b, 5)] = grad[b]
-        eo = even_odd([block[:, k] for k in range(5)])
-        tl, tr = line_traces(eo)
-        grad = line_apply(
-            eo,
-            pick(first_lane, tl, lanes_roll(tr, 1)),
-            pick(last_lane, tr, lanes_roll(tl, -1)),
-        )
-        for b in range(5):
-            gn[v, pl.ds(25 * a + 5 * b, 5)] = jnp.stack([grad[k][b] for k in range(5)])
-        return carry
-
-    lax.fori_loop(0, 25, local_ab, 0)
-
-    def local_c(k, carry):
-        v = k // 5
-        b = k - 5 * v
-        eo = even_odd([u[v, pl.ds(25 * a + 5 * b, 5)] for a in range(5)])
-        tl, tr = line_traces(eo)
-        q = 25 * v + 5 * b
-        tc[pl.ds(q, 5)] = pick(row_lo, tl, tr)
-        ucu[pl.ds(q, 5)] = tr[:, 6:8]
-        ucd[pl.ds(q, 5)] = tl[:, 0:2]
-        zero = jnp.zeros_like(tl)
-        grad = line_apply(
-            eo, pick(row_lo, zero, rows_roll(tr, 2)), pick(row_hi, zero, rows_roll(tl, -2))
-        )
+            term = span_trace[b][None] * u[v, pl.ds(25 * i + 5 * b, 5)]
+            acc = term if acc is None else acc + term
+        ts[pl.ds(q, 5)] = acc
+        acc = None
         for a in range(5):
-            gc[v, pl.ds(25 * a + 5 * b, 5)] = grad[a]
-        return carry
-
-    lax.fori_loop(0, 25, local_c, 0)
+            term = chord_trace[a][None] * u[v, pl.ds(25 * a + 5 * i, 5)]
+            acc = term if acc is None else acc + term
+        tc[pl.ds(q, 5)] = acc
+        ucu[pl.ds(q, 5)] = acc[:, 6:8]
+        ucd[pl.ds(q, 5)] = acc[:, 0:2]
+        return carry
+
+    lax.fori_loop(0, 25, outer_traces, 0)
     ts[125] = jnp.zeros((8, 128), jnp.float32)
     tsf[125] = jnp.zeros((8, 128), jnp.float32)
 
-    def pack(src, to_right, to_left, start, count):
+    def pack(src, to_right, to_left, first, count, step):
         def body(k, carry):
-            p = start + k * 1
-            two = src[pl.ds(2 * p, 2)]
-            to_right[p] = jnp.where(low_j, rows_roll(two[0], -1), two[1])
-            to_left[p] = jnp.where(low_j, two[0], rows_roll(two[1], 1))
+            p = first + step * k
+            two = src[pl.ds(2 * p, 2 * step)].reshape(step, 2, 8, 128)
+            one, other = two[:, 0], two[:, 1]
+            to_right[pl.ds(p, step)] = pick(low_j, rows_roll(one, -1), other)
+            to_left[pl.ds(p, step)] = pick(low_j, one, rows_roll(other, 1))
             return carry
 
-        lax.fori_loop(0, count, body, 0)
-
-    def unpack(from_left, from_right, p):
-        a, b = from_left[p], from_right[p]
-        return (
-            jnp.where(low_j, a, rows_roll(b, 1)),
-            jnp.where(low_j, rows_roll(a, -1), b),
-        )
-
-    pack(ts, usr, usl, 0, PAIRS)
-
-    pl.semaphore_wait(barrier, 2 + jnp.where(has_lo, 3, 0) + jnp.where(has_hi, 3, 0))
+        lax.fori_loop(0, count // step, body, 0)
+
+    pack(ts, usr, usl, 0, PAIRS, 9)
+
+    pl.semaphore_wait(barrier, 2 + jnp.where(has_lo, 3, 0) + jnp.where(has_hi, 3, 0) + extra)
 
     eps_copies = []
     for k, (dc, ds) in enumerate(SPOTS):
@@ -331,8 +340,8 @@
         guarded(exists(dc), copy.start)
         eps_copies.append((dc, ds, copy))
 
-    def exchange(bufs, sems, g):
-        (sr, sl, cu, cd), (dr, dl, du, dd) = bufs
+    def exchange(kind, g):
+        (sr, sl, cu, cd), (dr, dl, du, dd), sems = messages[kind]
         v0, v1 = GROUPS[g]
         pairs = pl.ds(25 * v0 // 2, -(-25 * (v1 - v0) // 2))
         lines = pl.ds(25 * v0, 25 * (v1 - v0))
@@ -353,32 +362,110 @@
                 device_id=(c_of[dc], s_of[ds]),
                 device_id_type=MESH,
             )
-            out.append((dc, copy))
+            first = None
+            if dc != 0 and (kind, g) in ROUTES:
+                t = ROUTES[(kind, g)]
+                n = RELAYS.index((kind, g))
+                crossing = is_up if dc == 1 else is_down
+                first = pltpu.make_async_remote_copy(
+                    src_ref=src.at[part],
+                    dst_ref=held.at[part],
+                    send_sem=sems[0].at[4 * g + k],
+                    recv_sem=h_recv.at[n],
+                    device_id=(t if dc == 1 else last - t, s),
+                    device_id_type=MESH,
+                )
+                second = pltpu.make_async_remote_copy(
+                    src_ref=held.at[part],
+                    dst_ref=dst.at[part],
+                    send_sem=h_send.at[n],
+                    recv_sem=sems[1].at[4 * g + k],
+                    device_id=(half if dc == 1 else half - 1, s),
+                    device_id_type=MESH,
+                )
+                first = (crossing, c == (t if dc == 1 else last - t), first, second)
+            out.append((dc, copy, first))
         return out
 
-    u_copies = [
-        exchange(((usr, usl, ucu, ucd), (vsr, vsl, vcu, vcd)), (u_send, u_recv), g)
-        for g in range(3)
-    ]
-    f_copies = [
-        exchange(((fsr, fsl, fcu, fcd), (hsr, hsl, hcu, hcd)), (f_send, f_recv), g)
-        for g in range(3)
-    ]
+    messages = {
+        "u": ((usr, usl, ucu, ucd), (vsr, vsl, vcu, vcd), (u_send, u_recv)),
+        "f": ((fsr, fsl, fcu, fcd), (hsr, hsl, hcu, hcd), (f_send, f_recv)),
+    }
+    u_copies = [exchange("u", g) for g in range(3)]
+    f_copies = [exchange("f", g) for g in range(3)]
 
     def start(copies):
-        for dc, copy in copies:
-            guarded(exists(dc), copy.start)
+        for dc, copy, relay in copies:
+            cond = exists(dc)
+            if relay is not None:
+                pl.when(relay[0])(relay[2].start)
+                cond = jnp.logical_and(cond, jnp.logical_not(relay[0]))
+            guarded(cond, copy.start)
+
+    def pass_on(copies):
+        for dc, copy, relay in copies:
+            if relay is not None:
+
+                def forward(relay=relay):
+                    relay[2].wait_recv()
+                    relay[3].start()
+
+                pl.when(relay[1])(forward)
 
     def arrive(copies):
-        for dc, copy in copies:
+        for dc, copy, relay in copies:
             guarded(exists(-dc), copy.wait_recv)
 
     def sent(copies):
-        for dc, copy in copies:
+        for dc, copy, relay in copies:
             guarded(exists(dc), copy.wait_send)
+            if relay is not None:
+                pl.when(relay[1])(relay[3].wait_send)
 
     for g in range(3):
         start(u_copies[g])
+
+    def local_ab(k, carry):
+        v = k // 5
+        a = k - 5 * v
+        block = u[v, pl.ds(25 * a, 25)].reshape(5, 5, 8, 128)
+        eo = even_odd([block[b] for b in range(5)])
+        tl, tr = line_traces(eo)
+        zero = jnp.zeros_like(tl)
+        grad = line_apply(
+            eo, pick(low_j, zero, rows_roll(tr, 1)), pick(low_j, rows_roll(tl, -1), zero)
+        )
+        for b in range(5):
+            gs[v, pl.ds(25 * a + 5 * b, 5)] = grad[b]
+        eo = even_odd([block[:, k] for k in range(5)])
+        tl, tr = line_traces(eo)
+        grad = line_apply(
+            eo,
+            pick(first_lane, tl, lanes_roll(tr, 1)),
+            pick(last_lane, tr, lanes_roll(tl, -1)),
+        )
+        for b in range(5):
+            gn[v, pl.ds(25 * a + 5 * b, 5)] = jnp.stack([grad[k][b] for k in range(5)])
+        return carry
+
+    lax.fori_loop(0, 25, local_ab, 0)
+
+    def local_c(k, carry):
+        v = k // 5
+        b = k - 5 * v
+        eo = even_odd([u[v, pl.ds(25 * a + 5 * b, 5)] for a in range(5)])
+        tl, tr = line_traces(eo)
+        zero = jnp.zeros_like(tl)
+        grad = line_apply(
+            eo, pick(row_lo, zero, rows_roll(tr, 2)), pick(row_hi, zero, rows_roll(tl, -2))
+        )
+        for a in range(5):
+            gc[v, pl.ds(25 * a + 5 * b, 5)] = grad[a]
+        return carry
+
+    lax.fori_loop(0, 25, local_c, 0)
+    for g in range(3):
+        pass_on(u_copies[g])
 
     for dc, ds, copy in eps_copies:
         guarded(exists(-dc), copy.wait_recv)
@@ -460,14 +547,6 @@
     for b in range(5):
         kc[pl.ds(5 * b, 5)] = jnp.stack(between(edge[0][b], edge[1][b]))
 
-    span_trace = [jnp.where(low_j, float(LEFT[b]), float(RIGHT[b])) for b in range(5)]
-    chord_trace = [jnp.where(row_lo, float(LEFT[a]), float(RIGHT[a])) for a in range(5)]
-    span_lift = [jnp.where(low_j, float(HALF_L[b]), float(HALF_R[b])) for b in range(5)]
-    chord_lift = [
-        jnp.where(row_lo, float(HALF_L[a]), jnp.where(row_hi, float(HALF_R[a]), 0.0))
-        for a in range(5)
-    ]
-
     def flux_traces(k, carry):
         v = k // 5
         a = k - 5 * v
@@ -489,7 +568,8 @@
 
     for g, (v0, v1) in enumerate(GROUPS):
         lax.fori_loop(5 * v0, 5 * v1, flux_traces, 0)
-        pack(tsf, fsr, fsl, 25 * v0 // 2, -(-25 * (v1 - v0) // 2))
+        count = -(-25 * (v1 - v0) // 2)
+        pack(tsf, fsr, fsl, 25 * v0 // 2, count, 5 if count % 5 == 0 else count)
         start(f_copies[g])
 
     def normal_part(k, carry):
@@ -513,15 +593,18 @@
     end_lo = jnp.logical_and(row_lo, jnp.logical_not(has_lo))
     end_hi = jnp.logical_and(row_hi, jnp.logical_not(has_hi))
 
-    def unpack_all(from_left, from_right, dst, start_pair, count):
+    def unpack(from_left, from_right, dst, first, count, step):
         def body(k, carry):
-            p = start_pair + k
-            first, second = unpack(from_left, from_right, p)
-            dst[2 * p] = first
-            dst[2 * p + 1] = second
+            p = first + step * k
+            a, b = from_left[pl.ds(p, step)], from_right[pl.ds(p, step)]
+            one = pick(low_j, a, rows_roll(b, 1))
+            other = pick(low_j, rows_roll(a, -1), b)
+            dst[pl.ds(2 * p, 2 * step)] = jnp.stack([one, other], axis=1).reshape(
+                2 * step, 8, 128
+            )
             return carry
 
-        lax.fori_loop(0, count, body, 0)
+        lax.fori_loop(0, count // step, body, 0)
 
     def chord_outer(from_lo, from_hi, q):
         lo = from_lo[pl.ds(q, 5)]
@@ -576,9 +659,11 @@
 
     for g, (v0, v1) in enumerate(GROUPS):
         arrive(u_copies[g])
-        unpack_all(vsr, vsl, tsf, 25 * v0 // 2, -(-25 * (v1 - v0) // 2))
+        count = -(-25 * (v1 - v0) // 2)
+        unpack(vsr, vsl, tsf, 25 * v0 // 2, count, 5 if count % 5 == 0 else count)
         lax.fori_loop(5 * v0, 5 * v1, span_part, 0)
         lax.fori_loop(5 * v0, 5 * v1, chord_part, 0)
+        pass_on(f_copies[g])
 
     def finish(k, carry):
         v = k // 5
@@ -603,7 +688,8 @@
 
     for g, (v0, v1) in enumerate(GROUPS):
         arrive(f_copies[g])
-        unpack_all(hsr, hsl, tsf, 25 * v0 // 2, -(-25 * (v1 - v0) // 2))
+        count = -(-25 * (v1 - v0) // 2)
+        unpack(hsr, hsl, tsf, 25 * v0 // 2, count, 5 if count % 5 == 0 else count)
         lax.fori_loop(5 * v0, 5 * v1, finish, 0)
         lax.fori_loop(5 * v0, 5 * v1, finish_chord, 0)
     for dc, ds, copy in eps_copies:
@@ -649,6 +735,7 @@
             pltpu.VMEM((126, 8, 128), f32),
         ]
         + [pairs, pairs, thin, thin] * 4
+        + [thin]
         + [
             pltpu.VMEM((8, 128), f32),
             pltpu.VMEM((8, 8, 128), f32),
@@ -661,6 +748,8 @@
             sem((12,)),
             sem((12,)),
             sem((12,)),
+            sem((len(RELAYS),)),
+            sem((len(RELAYS),)),
         ],
         compiler_params=pltpu.CompilerParams(
             collective_id=0, has_side_effects=True, vmem_limit_bytes=40 * 1024 * 1024

time: 32.1 us -> 26.3 us (0.82)
  Pallas kernels: 31.3 us -> 25.2 us
    pallas_call x1, Pallas kernels: 29.6 us -> 23.5 us  [shards(): pl.pallas_call(functools.partial(kernel, chords, spans), out_shape=(jax.S...]
where the time goes in v2:
time: 26.3 us; the launch traced here: 25.8 us
  Pallas kernels  25.2 us (96%)
  between operations  0.64 us (2%)
    pallas_call x1, Pallas kernels, shards(): pl.pallas_call(functools.partial(kernel, chords, spans), out_shape=(jax.S...  23.5 us
    pallas_call x1, Pallas kernels, shards(): pl.pallas_call(store_kernel, out_shape=(jax.ShapeDtypeStruct((5, 125, 8,...  1.68 us

profile of v2, /device:TPU:24, one launch (start us, length us, event | category | flops | bytes accessed | tf_op | source)
XLA Modules:
  0.0 25.8 jit_solution(12317926944076814352)
XLA Ops:
  0.6 23.5 %viscous.1 = (f32[5,125,8,128]{3,2,1,0:T(8,128)S(1)}, f32[125,8,128]{2,1,0:T(8,128)S(1)}) custom-call(f32[5,125,8,128]{3,2,1,0:T(8,128)} %bitcast.3), custom_call_target="tpu_custom_call" | custom-call | tf_op jit(solution)/shard_map/viscous/pallas_call | solution.py:719
  24.2 1.7 %store.1 = (f32[5,125,8,128]{3,2,1,0:T(8,128)}, f32[125,8,128]{2,1,0:T(8,128)}) custom-call(f32[5,125,8,128]{3,2,1,0:T(8,128)S(1)} %get-tuple-element.6.r, f32[125,8,128]{2,1,0:T(8,128)S(1)} %get-tuple-element.7.vis), custom_call_target="tpu_custom_call" | custom-call | tf_op jit(solution)/shard_map/store/pallas_call | solution.py:759

commit v3 on v2

--- a/solution.py
+++ b/solution.py
@@ -134,12 +134,25 @@
 SPOTS = tuple((dc, ds) for dc in (-1, 0, 1) for ds in (-1, 0, 1) if (dc, ds) != (0, 0))
 
 
+def lift_rows():
+    row = lax.broadcasted_iota(jnp.int32, (8, 128), 0)
+    low_j = lax.rem(row, 2) == 0
+    span = [jnp.where(low_j, float(HALF_L[b]), float(HALF_R[b])) for b in range(5)]
+    chord = [
+        jnp.where(row < 2, float(HALF_L[a]), jnp.where(row >= 6, float(HALF_R[a]), 0.0))
+        for a in range(5)
+    ]
+    return span, chord
+
+
 def kernel(
     chords,
     spans,
     x_hbm,
     r,
     vis,
+    out_s,
+    out_c,
     u,
     gs,
     gc,
@@ -195,6 +208,10 @@
         else:
             pl.when(cond)(action)
 
+    loads = [pltpu.make_async_copy(x_hbm.at[v], u.at[v], load_sem.at[v]) for v in range(5)]
+    for copy in loads:
+        copy.start()
+
     barrier = pltpu.get_barrier_semaphore()
     for dc, ds in SPOTS:
         guarded(
@@ -230,10 +247,6 @@
         extra = extra + meet(c == t, near + [half])
         near = [] if t == half - 2 else [half]
         extra = extra + meet(c == last - t, near + [half - 1])
-
-    loads = [pltpu.make_async_copy(x_hbm.at[v], u.at[v], load_sem.at[v]) for v in range(5)]
-    for copy in loads:
-        copy.start()
 
     row = lax.broadcasted_iota(jnp.int32, (8, 128), 0)
     lane = lax.broadcasted_iota(jnp.int32, (8, 128), 1)
@@ -284,11 +297,7 @@
 
     span_trace = [jnp.where(low_j, float(LEFT[b]), float(RIGHT[b])) for b in range(5)]
     chord_trace = [jnp.where(row_lo, float(LEFT[a]), float(RIGHT[a])) for a in range(5)]
-    span_lift = [jnp.where(low_j, float(HALF_L[b]), float(HALF_R[b])) for b in range(5)]
-    chord_lift = [
-        jnp.where(row_lo, float(HALF_L[a]), jnp.where(row_hi, float(HALF_R[a]), 0.0))
-        for a in range(5)
-    ]
+    span_lift, chord_lift = lift_rows()
 
     def outer_traces(k, carry):
         v = k // 5
@@ -665,11 +674,17 @@
         lax.fori_loop(5 * v0, 5 * v1, chord_part, 0)
         pass_on(f_copies[g])
 
+    def span_outer(q, at):
+        return tsf[pl.ds(q, 5)] + ks[pl.ds(at, 5)] * ts[pl.ds(q, 5)]
+
+    def chord_flux(q, at):
+        outer = chord_outer(hcu, hcd, q) + kc[pl.ds(at, 5)] * tc[pl.ds(q, 5)]
+        return pick(jnp.logical_or(end_lo, end_hi), jnp.zeros_like(outer), outer)
+
     def finish(k, carry):
         v = k // 5
         a = k - 5 * v
-        q = 25 * v + 5 * a
-        outer = tsf[pl.ds(q, 5)] + ks[pl.ds(5 * a, 5)] * ts[pl.ds(q, 5)]
+        outer = span_outer(25 * v + 5 * a, 5 * a)
         for b in range(5):
             at = pl.ds(25 * a + 5 * b, 5)
             r[v, at] = r[v, at] + span_lift[b][None] * outer
@@ -678,9 +693,7 @@
     def finish_chord(k, carry):
         v = k // 5
         b = k - 5 * v
-        q = 25 * v + 5 * b
-        outer = chord_outer(hcu, hcd, q) + kc[pl.ds(5 * b, 5)] * tc[pl.ds(q, 5)]
-        outer = pick(jnp.logical_or(end_lo, end_hi), jnp.zeros_like(outer), outer)
+        outer = chord_flux(25 * v + 5 * b, 5 * b)
         for a in range(5):
             at = pl.ds(25 * a + 5 * b, 5)
             r[v, at] = r[v, at] + chord_lift[a][None] * outer
@@ -690,8 +703,14 @@
         arrive(f_copies[g])
         count = -(-25 * (v1 - v0) // 2)
         unpack(hsr, hsl, tsf, 25 * v0 // 2, count, 5 if count % 5 == 0 else count)
-        lax.fori_loop(5 * v0, 5 * v1, finish, 0)
-        lax.fori_loop(5 * v0, 5 * v1, finish_chord, 0)
+        if g < 2:
+            lax.fori_loop(5 * v0, 5 * v1, finish, 0)
+            lax.fori_loop(5 * v0, 5 * v1, finish_chord, 0)
+        else:
+            for k in range(5):
+                at = pl.ds(5 * k, 5)
+                out_s[at] = span_outer(100 + 5 * k, 5 * k)
+                out_c[at] = chord_flux(100 + 5 * k, 5 * k)
     for dc, ds, copy in eps_copies:
         guarded(exists(dc), copy.wait_send)
     for g in range(3):
@@ -699,12 +718,22 @@
         sent(f_copies[g])
 
 
-def store_kernel(r, vis, res_hbm, vis_hbm, sem):
-    copies = [
-        pltpu.make_async_copy(r.at[v], res_hbm.at[v], sem.at[v]) for v in range(5)
-    ] + [pltpu.make_async_copy(vis, vis_hbm, sem.at[5])]
+def store_kernel(r, vis, out_s, out_c, res_hbm, vis_hbm, final, sem):
+    copies = [pltpu.make_async_copy(r.at[v], res_hbm.at[v], sem.at[v]) for v in range(4)]
+    copies.append(pltpu.make_async_copy(vis, vis_hbm, sem.at[5]))
     for copy in copies:
         copy.start()
+    span, chord = lift_rows()
+    for a in range(5):
+        for b in range(5):
+            at = pl.ds(25 * a + 5 * b, 5)
+            final[at] = (
+                r[4, at]
+                + span[b][None] * out_s[pl.ds(5 * a, 5)]
+                + chord[a][None] * out_c[pl.ds(5 * b, 5)]
+            )
+    copies.append(pltpu.make_async_copy(final, res_hbm.at[4], sem.at[4]))
+    copies[-1].start()
     for copy in copies:
         copy.wait()
 
@@ -716,14 +745,16 @@
     pairs = pltpu.VMEM((PAIRS, 8, 128), f32)
     thin = pltpu.VMEM((132, 2, 128), f32)
     sem = pltpu.SemaphoreType.DMA
-    partial, viscosity = pl.pallas_call(
+    partial, viscosity, out_s, out_c = pl.pallas_call(
         functools.partial(kernel, chords, spans),
         out_shape=(
             jax.ShapeDtypeStruct((5, 125, 8, 128), f32),
             jax.ShapeDtypeStruct((125, 8, 128), f32),
+            jax.ShapeDtypeStruct((25, 8, 128), f32),
+            jax.ShapeDtypeStruct((25, 8, 128), f32),
         ),
         in_specs=[pl.BlockSpec(memory_space=pltpu.HBM)],
-        out_specs=(pl.BlockSpec(memory_space=pltpu.VMEM), pl.BlockSpec(memory_space=pltpu.VMEM)),
+        out_specs=(pl.BlockSpec(memory_space=pltpu.VMEM),) * 4,
         scratch_shapes=[
             field,
             field,
@@ -762,12 +793,12 @@
             jax.ShapeDtypeStruct((5, 125, 8, 128), f32),
             jax.ShapeDtypeStruct((125, 8, 128), f32),
         ),
-        in_specs=[pl.BlockSpec(memory_space=pltpu.VMEM)] * 2,
+        in_specs=[pl.BlockSpec(memory_space=pltpu.VMEM)] * 4,
         out_specs=(pl.BlockSpec(memory_space=pl.ANY), pl.BlockSpec(memory_space=pl.ANY)),
-        scratch_shapes=[sem((6,))],
+        scratch_shapes=[pltpu.VMEM((125, 8, 128), f32), sem((6,))],
         compiler_params=pltpu.CompilerParams(vmem_limit_bytes=4 * 1024 * 1024),
         name="store",
-    )(partial, viscosity)
+    )(partial, viscosity, out_s, out_c)
     return residual.reshape(state.shape), viscosity.reshape(state.shape[1:])
 
 

time: 26.3 us -> 25.9 us (0.985)
  Pallas kernels: 25.2 us -> 24.8 us
    pallas_call x1, Pallas kernels: 23.5 us -> 23.1 us  [shards(): pl.pallas_call(functools.partial(kernel, chords, spans), out_shape=(jax.S...]
where the time goes in v3:
time: 25.9 us; the launch traced here: 25.4 us
  Pallas kernels  24.8 us (96%)
  between operations  0.64 us (2%)
    pallas_call x1, Pallas kernels, shards(): pl.pallas_call(functools.partial(kernel, chords, spans), out_shape=(jax.S...  23.1 us
    pallas_call x1, Pallas kernels, shards(): pl.pallas_call(store_kernel, out_shape=(jax.ShapeDtypeStruct((5, 125, 8,...  1.68 us

profile of v3, /device:TPU:24, one launch (start us, length us, event | category | flops | bytes accessed | tf_op | source)
XLA Modules:
  0.0 25.4 jit_solution(6517514965843267801)
XLA Ops:
  0.6 23.1 %viscous.1 = (f32[5,125,8,128]{3,2,1,0:T(8,128)S(1)}, f32[125,8,128]{2,1,0:T(8,128)S(1)}, f32[25,8,128]{2,1,0:T(8,128)S(1)}, f32[25,8,128]{2,1,0:T(8,128)S(1)}) custom-call(f32[5,125,8,128]{3,2,1,0:T(8,128)} %bitcast.3), custom_call_target="tpu_custom_call" | custom-call | tf_op jit(solution)/shard_map/viscous/pallas_call | solution.py:748
  23.8 1.7 %store.1 = (f32[5,125,8,128]{3,2,1,0:T(8,128)}, f32[125,8,128]{2,1,0:T(8,128)}) custom-call(f32[5,125,8,128]{3,2,1,0:T(8,128)S(1)} %get-tuple-element.8.r, f32[125,8,128]{2,1,0:T(8,128)S(1)} %get-tuple-element.9.vis, f32[25,8,128]{2,1,0:T(8,128)S(1)} %get-tuple-element.10.out_s, f32[25,8,128]{2,1,0:T(8,128)S(1)} %get-tuple-element.11.out_c), custom_call_target="tpu_custom_call" | custom-call | tf_op jit(solution)/shard_map/store/pallas_call | solution.py:790

commit v4 on v3

--- a/solution.py
+++ b/solution.py
@@ -129,6 +129,7 @@
 
 GROUPS = ((0, 2), (2, 4), (4, 5))
 PAIRS = 63
+PAD = 4
 ROUTES = {("u", 0): 0, ("u", 1): 1, ("u", 2): 2}
 RELAYS = tuple(ROUTES)
 SPOTS = tuple((dc, ds) for dc in (-1, 0, 1) for ds in (-1, 0, 1) if (dc, ds) != (0, 0))
@@ -313,8 +314,8 @@
             term = chord_trace[a][None] * u[v, pl.ds(25 * a + 5 * i, 5)]
             acc = term if acc is None else acc + term
         tc[pl.ds(q, 5)] = acc
-        ucu[pl.ds(q, 5)] = acc[:, 6:8]
-        ucd[pl.ds(q, 5)] = acc[:, 0:2]
+        ucu[pl.ds(PAD + q, 5)] = rows_roll(acc, 2)[:, 0:2]
+        ucd[pl.ds(PAD + q, 5)] = acc[:, 0:2]
         return carry
 
     lax.fori_loop(0, 25, outer_traces, 0)
@@ -353,7 +354,7 @@
         (sr, sl, cu, cd), (dr, dl, du, dd), sems = messages[kind]
         v0, v1 = GROUPS[g]
         pairs = pl.ds(25 * v0 // 2, -(-25 * (v1 - v0) // 2))
-        lines = pl.ds(25 * v0, 25 * (v1 - v0))
+        lines = pl.ds(PAD + 25 * v0, 25 * (v1 - v0))
         out = []
         for k, (src, dst, dc, ds, part) in enumerate(
             (
@@ -571,8 +572,8 @@
             term = chord_trace[i][None] * (vis[at[i]] * gc[v, at[i]])
             acc = term if acc is None else acc + term
         q = 25 * v + 5 * a
-        fcu[pl.ds(q, 5)] = acc[:, 6:8]
-        fcd[pl.ds(q, 5)] = acc[:, 0:2]
+        fcu[pl.ds(PAD + q, 5)] = rows_roll(acc, 2)[:, 0:2]
+        fcd[pl.ds(PAD + q, 5)] = acc[:, 0:2]
         return carry
 
     for g, (v0, v1) in enumerate(GROUPS):
@@ -616,8 +617,8 @@
         lax.fori_loop(0, count // step, body, 0)
 
     def chord_outer(from_lo, from_hi, q):
-        lo = from_lo[pl.ds(q, 5)]
-        hi = from_hi[pl.ds(q, 5)]
+        lo = from_lo[pl.ds(PAD + q, 5)]
+        hi = from_hi[pl.ds(PAD + q, 5)]
         gap = jnp.zeros((5, 4, 128), jnp.float32)
         return jnp.concatenate([lo, gap, hi], axis=1)
 
@@ -743,7 +744,7 @@
     f32 = jnp.float32
     field = pltpu.VMEM((5, 125, 8, 128), f32)
     pairs = pltpu.VMEM((PAIRS, 8, 128), f32)
-    thin = pltpu.VMEM((132, 2, 128), f32)
+    thin = pltpu.VMEM((125 + 2 * PAD, 2, 128), f32)
     sem = pltpu.SemaphoreType.DMA
     partial, viscosity, out_s, out_c = pl.pallas_call(
         functools.partial(kernel, chords, spans),

time: 25.9 us -> 25.9 us (level)
  no operation moved by 1% of the time
where the time goes in v4:
time: 25.9 us; the launch traced here: 25.5 us
  Pallas kernels  24.8 us (96%)
  between operations  0.64 us (2%)
    pallas_call x1, Pallas kernels, shards(): pl.pallas_call(functools.partial(kernel, chords, spans), out_shape=(jax.S...  23.1 us
    pallas_call x1, Pallas kernels, shards(): pl.pallas_call(store_kernel, out_shape=(jax.ShapeDtypeStruct((5, 125, 8,...  1.68 us

profile of v4, /device:TPU:24, one launch (start us, length us, event | category | flops | bytes accessed | tf_op | source)
XLA Modules:
  0.0 25.5 jit_solution(1807667746418061921)
XLA Ops:
  0.6 23.1 %viscous.1 = (f32[5,125,8,128]{3,2,1,0:T(8,128)S(1)}, f32[125,8,128]{2,1,0:T(8,128)S(1)}, f32[25,8,128]{2,1,0:T(8,128)S(1)}, f32[25,8,128]{2,1,0:T(8,128)S(1)}) custom-call(f32[5,125,8,128]{3,2,1,0:T(8,128)} %bitcast.3), custom_call_target="tpu_custom_call" | custom-call | tf_op jit(solution)/shard_map/viscous/pallas_call | solution.py:749
  23.8 1.7 %store.1 = (f32[5,125,8,128]{3,2,1,0:T(8,128)}, f32[125,8,128]{2,1,0:T(8,128)}) custom-call(f32[5,125,8,128]{3,2,1,0:T(8,128)S(1)} %get-tuple-element.8.r, f32[125,8,128]{2,1,0:T(8,128)S(1)} %get-tuple-element.9.vis, f32[25,8,128]{2,1,0:T(8,128)S(1)} %get-tuple-element.10.out_s, f32[25,8,128]{2,1,0:T(8,128)S(1)} %get-tuple-element.11.out_c), custom_call_target="tpu_custom_call" | custom-call | tf_op jit(solution)/shard_map/store/pallas_call | solution.py:791
